TPU v7x, 32 devices: a whole 2x2x4 slice. The times are simulated.
32 devices in a mesh: dp: 4 (over z), ctx: 4 (over y, core), tp: 2 (over x).
Axes of the slice: x: 2, y: 2, z: 4, core: 2. Of those that a mesh axis runs over, the one named last changes fastest.
Arguments:
- hidden: bfloat16 [4, 512, 4096], P('dp', 'ctx'), may hold values from -6 to 6
- query_heads: bfloat16 [4, 512, 4096], P('dp', 'ctx', 'tp'), may hold values from -6 to 6
- key_heads: bfloat16 [4, 512, 512], P('dp', 'ctx', 'tp'), may hold values from -6 to 6
- value_heads: bfloat16 [4, 512, 512], P('dp', 'ctx', 'tp'), may hold values from -6 to 6
- attention_out: bfloat16 [4, 512, 4096], P('dp', 'ctx', 'tp'), may hold values from -3 to 3
- output_grad: bfloat16 [4, 512, 4096], P('dp', 'ctx', 'tp'), may hold values from -3 to 3
- log_norm: float32 [4, 32, 512], P('dp', 'tp', 'ctx'), may hold values from -40 to 40, as said below
- block_order: int32 [8], replicated, may hold values from 0 to 7, as said below
- value_weight: bfloat16 [4096, 512], P(None, 'tp'), may hold values from -0.25 to 0.25
Outputs:
- query_grad: bfloat16 [4, 512, 4096], P('dp', 'ctx', 'tp')
- key_grad: bfloat16 [4, 512, 512], P('dp', 'ctx', 'tp')
- value_grad: bfloat16 [4, 512, 512], P('dp', 'ctx', 'tp')
- hidden_grad: bfloat16 [4, 512, 4096], P('dp', 'ctx', 'tp')
- weight_grad: float32 [4096, 512], P('ctx', 'tp')
Inputs may be any that keep to these rules, and one draw needn't show every extreme that they name: `block_order`: each of 0 to 7 once. log_norm is the log of the sum of exp(scores) over the keys visible to that row, so the probabilities of each row and head sum to one.
All inputs are finite; a program needn't handle non-finite values.
Results may differ from a plain program's by a relative error of at most 0.025.
Values may be sent and summed in bfloat16 or wider, within the bound.
A program may use at most 64 MiB of HBM per device.

v0:
```python
import math
import jax
import jax.numpy as jnp
from jax import lax
from jax.sharding import PartitionSpec as P

HD = 128
HQ = 32
KVH = 4


def block_positions(row_ids, block_order, block_len):
    labels = jnp.arange(block_order.shape[0], dtype=jnp.int32)
    picked = jnp.where((row_ids // block_len)[:, None] == labels[None, :], block_order[None, :], 0)
    return jnp.sum(picked, axis=1) * block_len + row_ids % block_len


def shards(
    hidden,
    query_heads,
    key_heads,
    value_heads,
    attention_out,
    output_grad,
    log_norm,
    block_order,
    value_weight,
):
    tokens = query_heads.shape[1]
    local_heads = key_heads.shape[2] // HD
    members = HQ // KVH
    block_len = tokens // 2
    cycle_size = lax.axis_size("ctx")
    cycle_rank = lax.axis_index("ctx")
    score_scale = HD ** (-0.5)
    local_rows = cycle_rank * tokens + jnp.arange(tokens, dtype=jnp.int32)
    query_pos = block_positions(local_rows, block_order, block_len)
    query_rows = query_heads[0].reshape(tokens, local_heads, members, HD)
    out_rows = attention_out[0].reshape(tokens, local_heads, members, HD)
    grad_rows = output_grad[0].reshape(tokens, local_heads, members, HD)
    row_delta = jnp.einsum(
        "tgjd,tgjd->gjt", grad_rows, out_rows, preferred_element_type=jnp.float32
    )
    norm_rows = log_norm[0].reshape(local_heads, members, tokens)

    def attend(running, key_block, value_block, block_first):
        key_count = key_block.shape[0]
        key_ids = block_first + jnp.arange(key_count, dtype=jnp.int32)
        key_pos = block_positions(key_ids, block_order, block_len)
        visible = key_pos[None, :] <= query_pos[:, None]
        acc_query, acc_key, acc_value = running
        scores = (
            jnp.einsum("tgjd,kgd->gjtk", query_rows, key_block, preferred_element_type=jnp.float32)
            * score_scale
        )
        shifted = jnp.where(visible[None, None], scores - norm_rows[:, :, :, None], -jnp.inf)
        probability = jnp.exp(shifted)
        weights = probability.astype(jnp.bfloat16)
        fresh_value = jnp.einsum(
            "gjtk,tgjd->kgd", weights, grad_rows, preferred_element_type=jnp.float32
        )
        through = jnp.einsum(
            "tgjd,kgd->gjtk", grad_rows, value_block, preferred_element_type=jnp.float32
        )
        slopes = (probability * (through - row_delta[:, :, :, None])).astype(jnp.bfloat16)
        acc_query = acc_query + jnp.einsum(
            "gjtk,kgd->tgjd", slopes, key_block, preferred_element_type=jnp.float32
        )
        fresh_key = jnp.einsum(
            "gjtk,tgjd->kgd", slopes, query_rows, preferred_element_type=jnp.float32
        )
        acc_key = lax.dynamic_update_slice_in_dim(
            acc_key,
            lax.dynamic_slice_in_dim(acc_key, block_first, key_count, 0) + fresh_key,
            block_first,
            0,
        )
        acc_value = lax.dynamic_update_slice_in_dim(
            acc_value,
            lax.dynamic_slice_in_dim(acc_value, block_first, key_count, 0) + fresh_value,
            block_first,
            0,
        )
        return (acc_query, acc_key, acc_value)

    def accumulate(running, pieces, first_row):
        key_piece, value_piece = pieces
        key_count = key_piece.shape[0]
        sub_width = math.gcd(key_count, 512)
        sub_turns = key_count // sub_width
        if sub_turns == 1:
            return attend(running, key_piece, value_piece, first_row)

        def advance(step_index, inner_state):
            offset = step_index * sub_width
            return attend(
                inner_state,
                lax.dynamic_slice_in_dim(key_piece, offset, sub_width, 0),
                lax.dynamic_slice_in_dim(value_piece, offset, sub_width, 0),
                first_row + offset,
            )

        return lax.fori_loop(0, sub_turns, advance, running)

    zeros_query = jnp.zeros((tokens, local_heads, members, HD), jnp.float32)
    zeros_pair = jnp.zeros((cycle_size * tokens, local_heads, HD), jnp.float32)
    key_local = key_heads[0].reshape(tokens, local_heads, HD)
    value_local = value_heads[0].reshape(tokens, local_heads, HD)
    acc_query, part_key, part_value = accumulate(
        (zeros_query, zeros_pair, zeros_pair),
        (
            lax.all_gather(key_local, "ctx", axis=0, tiled=True),
            lax.all_gather(value_local, "ctx", axis=0, tiled=True),
        ),
        jnp.int32(0),
    )
    own_key, own_value = (
        lax.psum_scatter(
            part_key.astype(jnp.bfloat16), "ctx", scatter_dimension=0, tiled=True
        ).astype(jnp.float32),
        lax.psum_scatter(
            part_value.astype(jnp.bfloat16), "ctx", scatter_dimension=0, tiled=True
        ).astype(jnp.float32),
    )
    query_grad = (
        (acc_query * score_scale)
        .astype(jnp.bfloat16)
        .reshape(1, tokens, local_heads * members * HD)
    )
    key_grad = (own_key * score_scale).astype(jnp.bfloat16).reshape(1, tokens, local_heads * HD)
    value_grad = own_value.astype(jnp.bfloat16).reshape(1, tokens, local_heads * HD)
    value_rows = value_grad[0]
    inputs = hidden[0]
    partial_term = jnp.einsum("td,te->de", inputs, value_rows, preferred_element_type=jnp.float32)
    row_share = lax.psum_scatter(
        lax.optimization_barrier(partial_term.astype(jnp.bfloat16))
        .astype(jnp.float32)
        .astype(jnp.bfloat16),
        "ctx",
        scatter_dimension=0,
        tiled=True,
    )
    summed_rows = lax.psum(row_share, "dp").astype(jnp.float32)
    token_norm = (lax.axis_size("dp") * cycle_size * tokens) ** (-0.5)
    weight_grad = summed_rows * token_norm
    partial_value = jnp.einsum(
        "te,de->td", value_rows, value_weight, preferred_element_type=jnp.float32
    )
    summed = lax.psum_scatter(
        partial_value.astype(jnp.bfloat16), "tp", scatter_dimension=1, tiled=True
    ).astype(jnp.float32)
    hidden_grad = summed.astype(jnp.bfloat16).reshape(1, tokens, summed.shape[1])
    return (query_grad, key_grad, value_grad, hidden_grad, weight_grad)


def solution(mesh):
    placed = (
        P("dp", "ctx", None),
        P("dp", "ctx", "tp"),
        P("dp", "ctx", "tp"),
        P("dp", "ctx", "tp"),
        P("dp", "ctx", "tp"),
        P("dp", "ctx", "tp"),
        P("dp", "tp", "ctx"),
        P(),
        P(None, "tp"),
    )
    return jax.shard_map(
        shards,
        mesh=mesh,
        in_specs=placed,
        out_specs=(
            P("dp", "ctx", "tp"),
            P("dp", "ctx", "tp"),
            P("dp", "ctx", "tp"),
            P("dp", "ctx", "tp"),
            P("ctx", "tp"),
        ),
        check_vma=False,
    )
```

profile of v0, /device:TPU:0, one launch (start us, length us, event | category | flops | bytes accessed | tf_op | source)
XLA Modules:
  0.0 174.6 jit_solution(1316045915267573734)
XLA Ops:
  7.2 0.0 copy-start
  7.2 0.0 copy-start.5
  7.2 0.0 reduce-scatter.7.cloned.1.call-start
  7.3 0.9 select_reduce_fusion.1
  8.2 0.7 select_reduce_fusion
  8.9 0.9 copy.39
  9.9 0.1 copy.40
  10.0 7.3 %all_gather.6 = bf16[512,2,128]{2,0,1:T(8,128)(2,1)S(1)} all-gather(bf16[128,2,128]{2,0,1:T(8,128)(2,1)S(1)} %copy.40), channel_id=1, replica_groups=mesh['dp'=4,'ctx'=4,'tp'=2] {'ctx'}, dimensions={0}, use_global_device_ids=true | all-gather | bytes 327680 | tf_op jit(solution)/shard_map/all_gather | solution.py:112
  17.2 1.1 copy.72
  18.4 1.1 copy.73
  19.5 0.1 broadcast_compare_fusion
  19.7 0.0 copy-start.4
  19.7 0.7 fusion.26
  20.4 0.0 copy-start.1
  20.4 1.9 %copy-done.1 = f32[2,512,128,8]{2,1,3,0:T(8,128)} copy-done((f32[2,512,128,8]{2,1,3,0:T(8,128)}, f32[2,512,128,8]{2,1,3,0:T(8,128)S(1)}, u32[]{:S(2)}) %copy-start.1) | copy-done | bytes 4194328
  22.3 0.0 copy-done.5
  22.3 1.7 %fusion.17 = bf16[512,2,128]{2,0,1:T(8,128)(2,1)} fusion(f32[2,512,128,8]{2,1,3,0:T(8,128)S(1)} %fusion.26, f32[2,8,128]{2,1,0:T(8,128)S(1)} %bitcast.109, pred[128,512]{0,1:T(8,128)(4,1)S(1)} %broadcast_compare_fusion, bf16[128,2,8,128]{3,2,1,0:T(8,128)(2,1)S(1)} %bitcast.94), kind=kOutput, calls=%fused_computation.18 | convolution fusion | flops 272760832 | bytes 5054464 | tf_op jit(solution)/shard_map/gjtk,tgjd->kgd/dot_general | solution.py:59
  24.1 0.0 copy-done.4
  24.1 0.0 copy-start.3
  24.1 0.0 reduce-scatter.7.cloned.1.call-update
  24.1 0.0 reduce-scatter.11.cloned.1.call-start
  24.2 21.4 %reduce-scatter.7.cloned.1.call-done = bf16[128,2,128]{2,0,1:T(8,128)(2,1)} async-done(((bf16[512,2,128]{2,0,1:T(8,128)(2,1)}), bf16[128,2,128]{2,0,1:T(8,128)(2,1)}) %reduce-scatter.7.cloned.1.call-update) | async-done | bytes 65552 | tf_op jit(solution)/shard_map/reduce_scatter | solution.py:121
  45.6 0.9 copy.50
  46.6 3.3 %fusion = bf16[4096,256]{0,1:T(8,128)(2,1)} fusion(bf16[128,256]{0,1:T(8,128)(2,1)S(1)} %bitcast.99, bf16[1,128,4096]{2,1,0:T(8,128)(2,1)} %param.9), kind=kOutput, calls=%fused_computation.1 | convolution fusion | flops 269484032 | bytes 3211264 | tf_op jit(solution)/shard_map/td,te->de/dot_general | solution.py:134
  49.8 0.0 reduce-scatter.11.cloned.1.call-update
  49.8 0.0 reduce-scatter.5.cloned.1.call-start
  49.9 0.0 copy-done.3
  49.9 0.7 copy.42
  50.6 0.9 copy.43
  51.6 1.2 copy.74
  52.8 1.1 fusion.22
  53.9 1.0 copy.64
  54.8 5.8 %all_gather.7 = bf16[512,2,128]{2,0,1:T(8,128)(2,1)S(1)} all-gather(bf16[128,2,128]{2,0,1:T(8,128)(2,1)S(1)} %copy.43), channel_id=1, replica_groups=mesh['dp'=4,'ctx'=4,'tp'=2] {'ctx'}, dimensions={0}, use_global_device_ids=true | all-gather | bytes 327680 | tf_op jit(solution)/shard_map/all_gather | solution.py:113
  60.6 3.6 %fusion.2 = bf16[2,8,128,512]{2,3,1,0:T(8,128)(2,1)S(1)} fusion(f32[2,512,128,8]{2,1,3,0:T(8,128)} %copy-done.1, f32[2,8,128]{2,1,0:T(8,128)S(1)} %copy.64, f32[2,8,128]{2,1,0:T(8,128)S(1)} %bitcast.110, pred[128,512]{0,1:T(8,128)(4,1)} %copy-done.4, bf16[128,2,8,128]{3,2,1,0:T(8,128)(2,1)S(1)} %bitcast.96, bf16[512,2,128]{2,0,1:T(8,128)(2,1)S(1)} %all_gather.7), kind=kOutput, calls=%fused_computation.5 | convolution fusion | flops 274726912 | bytes 7159808 | tf_op jit(solution)/shard_map/tgjd,kgd->gjtk/dot_general | solution.py:62
  64.2 0.0 copy-start.2
  64.2 1.3 copy-done.2
  65.6 1.4 fusion.20
  67.0 0.0 reduce-scatter.5.cloned.1.call-update
  67.0 0.0 all-reduce.2.cloned.1.call-start
  67.1 14.1 %reduce-scatter.11.cloned.1.call-done = bf16[1024,256]{0,1:T(8,128)(2,1)} async-done(((bf16[4096,256]{0,1:T(8,128)(2,1)}), bf16[1024,256]{0,1:T(8,128)(2,1)}) %reduce-scatter.11.cloned.1.call-update) | async-done | bytes 524304 | tf_op jit(solution)/shard_map/reduce_scatter | solution.py:135
  81.2 0.0 all-reduce.2.cloned.1.call-update
  81.2 0.0 reduce-scatter.9.cloned.1.call-start
  81.3 0.0 copy-done
  81.3 1.8 %convolution_convert_fusion.1 = bf16[128,4096]{1,0:T(8,128)(2,1)} fusion(bf16[128,256]{0,1:T(8,128)(2,1)S(1)} %bitcast.100, bf16[4096,256]{1,0:T(8,128)(2,1)S(1)} %copy-done), kind=kOutput, calls=%fused_computation.2 | convolution fusion | flops 268959744 | bytes 3211264 | tf_op jit(solution)/shard_map/te,de->td/dot_general | solution.py:146
  83.1 0.0 reduce-scatter.9.cloned.1.call-update
  83.1 2.1 %fusion.9 = bf16[2,8,128,128]{2,3,1,0:T(8,128)(2,1)S(1)} fusion(bf16[2,8,128,512]{2,3,1,0:T(8,128)(2,1)} %copy-done.2, bf16[512,2,128]{2,0,1:T(8,128)(2,1)S(1)} %all_gather.6), kind=kOutput, calls=%fused_computation.13 | convolution fusion | flops 268959744 | bytes 2883584 | tf_op jit(solution)/shard_map/gjtk,kgd->tgjd/dot_general | solution.py:66
  85.2 1.0 copy.52
  86.2 18.1 %reduce-scatter.5.cloned.1.call-done = bf16[128,2,128]{2,0,1:T(8,128)(2,1)} async-done(((bf16[512,2,128]{2,0,1:T(8,128)(2,1)}), bf16[128,2,128]{2,0,1:T(8,128)(2,1)}) %reduce-scatter.5.cloned.1.call-update) | async-done | bytes 65552 | tf_op jit(solution)/shard_map/reduce_scatter | solution.py:118
  104.3 0.9 multiply_convert_fusion
  105.2 0.1 copy.48
  105.3 0.7 copy.53
  106.0 0.7 copy.54
  106.8 38.4 %all-reduce.2.cloned.1.call-done = bf16[1024,256]{0,1:T(8,128)(2,1)} async-done(((bf16[1024,256]{0,1:T(8,128)(2,1)}), bf16[1024,256]{0,1:T(8,128)(2,1)}) %all-reduce.2.cloned.1.call-update) | async-done | bytes 524304 | tf_op jit(solution)/shard_map/psum | solution.py:143
  145.2 1.2 convert_multiply_fusion.1
  146.4 1.3 copy.55
  147.7 20.4 %reduce-scatter.9.cloned.1.call-done = bf16[128,2048]{1,0:T(8,128)(2,1)} async-done(((bf16[128,4096]{1,0:T(8,128)(2,1)}), bf16[128,2048]{1,0:T(8,128)(2,1)}) %reduce-scatter.9.cloned.1.call-update) | async-done | bytes 524304 | tf_op jit(solution)/shard_map/reduce_scatter | solution.py:149
  (4 shorter events, 0.0 us)
Async XLA Ops:
  7.2 74.1 %copy-start = (bf16[4096,256]{1,0:T(8,128)(2,1)S(1)}, bf16[4096,256]{1,0:T(8,128)(2,1)}, u32[]{:S(2)}) copy-start(bf16[4096,256]{1,0:T(8,128)(2,1)} %param.17) | copy-start | bytes 6291460
  7.2 15.2 %copy-start.5 = (f32[1,16,128]{2,1,0:T(8,128)S(1)}, f32[1,16,128]{2,1,0:T(8,128)}, u32[]{:S(2)}) copy-start(f32[1,16,128]{2,1,0:T(8,128)} %param.15) | copy-start | bytes 24580
  7.2 38.4 %reduce-scatter.7.cloned.1.call-start = ((), (), s32[]{:S(2)}) async-start(), calls=%async_computation.5 | async-start | bytes 327680 | tf_op jit(solution)/shard_map/reduce_scatter | solution.py:121
  19.7 4.4 %copy-start.4 = (pred[128,512]{0,1:T(8,128)(4,1)}, pred[128,512]{0,1:T(8,128)(4,1)S(1)}, u32[]{:S(2)}) copy-start(pred[128,512]{0,1:T(8,128)(4,1)S(1)} %broadcast_compare_fusion) | copy-start | bytes 196612
  20.4 1.9 %copy-start.1 = (f32[2,512,128,8]{2,1,3,0:T(8,128)}, f32[2,512,128,8]{2,1,3,0:T(8,128)S(1)}, u32[]{:S(2)}) copy-start(f32[2,512,128,8]{2,1,3,0:T(8,128)S(1)} %fusion.26) | copy-start | bytes 12582916
  24.1 25.8 %copy-start.3 = (bf16[1,128,256]{2,1,0:T(8,128)(2,1)S(1)}, bf16[1,128,256]{2,1,0:T(8,128)(2,1)}, u32[]{:S(2)}) copy-start(bf16[1,128,256]{2,1,0:T(8,128)(2,1)} %param.12) | copy-start | bytes 196612
  24.1 57.1 %reduce-scatter.11.cloned.1.call-start = ((), (), s32[]{:S(2)}) async-start(), calls=%async_computation.7 | async-start | bytes 2621440 | tf_op jit(solution)/shard_map/reduce_scatter | solution.py:135
  49.8 54.5 %reduce-scatter.5.cloned.1.call-start = ((), (), s32[]{:S(2)}) async-start(), calls=%async_computation.4 | async-start | bytes 327680 | tf_op jit(solution)/shard_map/reduce_scatter | solution.py:118
  64.2 1.4 copy-start.2
  67.0 78.2 %all-reduce.2.cloned.1.call-start = ((), (), s32[]{:S(2)}) async-start(), calls=%async_computation.8 | async-start | bytes 1048576 | tf_op jit(solution)/shard_map/psum | solution.py:143
  81.2 86.9 %reduce-scatter.9.cloned.1.call-start = ((), (), s32[]{:S(2)}) async-start(), calls=%async_computation.6 | async-start | bytes 1572864 | tf_op jit(solution)/shard_map/reduce_scatter | solution.py:149
Sparse Core Ops, SparseCore 0:
  24.2 21.3 reduce-scatter.6
  50.0 31.1 reduce-scatter.10
  84.2 20.0 reduce-scatter.4
  106.5 38.6 all-reduce.1
  147.9 20.1 reduce-scatter.8
where the time goes:
time: 175 us
  waiting for transfers between devices  113 us (65%)
  local copies, waits for them, and re-layouts  15.3 us (9%)
  matrix products  14.6 us (8%)
  between operations  14 us (8%)
  blocking collectives  13 us (7%)
  other arithmetic  4.91 us (3%)
    psum x1, waiting for transfers between devices, shards(): summed_rows = lax.psum(row_share, 'dp').astype(jnp.float32)  38.4 us
    reduce_scatter x1, waiting for transfers between devices, shards(): lax.psum_scatter(part_value.astype(jnp.bfloat16), 'ctx', scatter_dimensio...  21.4 us
    reduce_scatter x1, waiting for transfers between devices, shards(): lax.psum_scatter(partial_value.astype(jnp.bfloat16), 'tp', scatter_dimens...  20.4 us
    reduce_scatter x1, waiting for transfers between devices, shards(): lax.psum_scatter(part_key.astype(jnp.bfloat16), 'ctx', scatter_dimension=...  18.1 us
    reduce_scatter x1, waiting for transfers between devices, shards(): lax.psum_scatter(lax.optimization_barrier(partial_term.astype(jnp.bfloat1...  14.1 us
    unnamed x21, local copies, waits for them, and re-layouts  12.2 us
    all_gather x1, blocking collectives, shards(): lax.all_gather(key_local, 'ctx', axis=0, tiled=True)  7.25 us
    all_gather x1, blocking collectives, shards(): lax.all_gather(value_local, 'ctx', axis=0, tiled=True)  5.78 us
  transfers between devices with their start and end apart: 5, of which 5 were waited for; matrix products, arithmetic and copies ran while one was open for 11% of the time, Pallas kernels for 0%

commit v1 on v0

--- a/solution.py
+++ b/solution.py
@@ -140,7 +140,7 @@
         scatter_dimension=0,
         tiled=True,
     )
-    summed_rows = lax.psum(row_share, "dp").astype(jnp.float32)
+    summed_rows = jnp.sum(lax.all_gather(row_share, "dp"), axis=0).astype(jnp.float32)
     token_norm = (lax.axis_size("dp") * cycle_size * tokens) ** (-0.5)
     weight_grad = summed_rows * token_norm
     partial_value = jnp.einsum(

time: 175 us -> 181 us (1.034)
  waiting for transfers between devices: 113 us -> 108 us
  other arithmetic: 4.91 us -> 9.85 us
  local copies, waits for them, and re-layouts: 15.3 us -> 19.8 us
    all_gather x0 -> x1, waiting for transfers between devices: none -> 44.6 us  [shards(): lax.all_gather(row_share, 'dp')]
    psum x1 -> x0, waiting for transfers between devices: 38.4 us -> none  [shards(): summed_rows = lax.psum(row_share, 'dp').astype(jnp.float32)]
    reduce_scatter x1, waiting for transfers between devices: 20.4 us -> 9.99 us  [shards(): lax.psum_scatter(partial_value.astype(jnp.bfloat16), 'tp', scatter_dimens...]
    reduce_sum x0 -> x1, other arithmetic: none -> 4.93 us  [shards(): jnp.sum(lax.all_gather(row_share, 'dp'), axis=0).astype(jnp.float32)]
    all_gather x0 -> x1, local copies, waits for them, and re-layouts: none -> 4.51 us  [shards(): lax.all_gather(row_share, 'dp')]
  transfers between devices with their start and end apart: 5 -> 5, of which waited for: 5 -> 5; matrix products, arithmetic and copies ran while one was open for 11% -> 16% of each run, Pallas kernels for 0% -> 0%
where the time goes in v1:
time: 181 us; the launch traced here: 180 us
  waiting for transfers between devices  108 us (60%)
  local copies, waits for them, and re-layouts  19.8 us (11%)
  matrix products  14.6 us (8%)
  between operations  14 us (8%)
  blocking collectives  13 us (7%)
  other arithmetic  9.85 us (5%)
    all_gather x1, waiting for transfers between devices, shards(): lax.all_gather(row_share, 'dp')  44.6 us
    reduce_scatter x1, waiting for transfers between devices, shards(): lax.psum_scatter(part_value.astype(jnp.bfloat16), 'ctx', scatter_dimensio...  21.4 us
    reduce_scatter x1, waiting for transfers between devices, shards(): lax.psum_scatter(part_key.astype(jnp.bfloat16), 'ctx', scatter_dimension=...  18.1 us
    reduce_scatter x1, waiting for transfers between devices, shards(): lax.psum_scatter(lax.optimization_barrier(partial_term.astype(jnp.bfloat1...  14.2 us
    unnamed x21, local copies, waits for them, and re-layouts  12.1 us
    reduce_scatter x1, waiting for transfers between devices, shards(): lax.psum_scatter(partial_value.astype(jnp.bfloat16), 'tp', scatter_dimens...  9.99 us
    all_gather x1, blocking collectives, shards(): lax.all_gather(key_local, 'ctx', axis=0, tiled=True)  7.25 us
    all_gather x1, blocking collectives, shards(): lax.all_gather(value_local, 'ctx', axis=0, tiled=True)  5.78 us
  transfers between devices with their start and end apart: 5, of which 5 were waited for; matrix products, arithmetic and copies ran while one was open for 16% of the time, Pallas kernels for 0%

profile of v1, /device:TPU:0, one launch (start us, length us, event | category | flops | bytes accessed | tf_op | source)
XLA Modules:
  0.0 179.8 jit_solution(16315202299684812930)
XLA Ops:
  7.2 0.0 copy-start
  7.2 0.0 copy-start.5
  7.2 0.0 reduce-scatter.7.cloned.1.call-start
  7.3 0.9 select_reduce_fusion.1
  8.2 0.7 select_reduce_fusion
  8.9 0.9 copy.54
  9.9 0.1 copy.55
  10.0 7.3 %all_gather.12 = bf16[512,2,128]{2,0,1:T(8,128)(2,1)S(1)} all-gather(bf16[128,2,128]{2,0,1:T(8,128)(2,1)S(1)} %copy.55), channel_id=1, replica_groups=mesh['dp'=4,'ctx'=4,'tp'=2] {'ctx'}, dimensions={0}, use_global_device_ids=true | all-gather | bytes 327680 | tf_op jit(solution)/shard_map/all_gather | solution.py:112
  17.2 1.1 copy.87
  18.4 1.1 copy.88
  19.5 0.1 broadcast_compare_fusion
  19.7 0.0 copy-start.4
  19.7 0.7 fusion.26
  20.4 0.0 copy-start.1
  20.4 0.0 copy-done.4
  20.4 1.9 %copy-done.1 = f32[2,512,128,8]{2,1,3,0:T(8,128)} copy-done((f32[2,512,128,8]{2,1,3,0:T(8,128)}, f32[2,512,128,8]{2,1,3,0:T(8,128)S(1)}, u32[]{:S(2)}) %copy-start.1) | copy-done | bytes 4194328
  22.3 0.0 copy-done.5
  22.3 1.7 fusion.17
  24.1 0.0 copy-start.3
  24.1 0.0 reduce-scatter.7.cloned.1.call-update
  24.1 0.0 reduce-scatter.11.cloned.1.call-start
  24.2 21.4 %reduce-scatter.7.cloned.1.call-done = bf16[128,2,128]{2,0,1:T(8,128)(2,1)} async-done(((bf16[512,2,128]{2,0,1:T(8,128)(2,1)}), bf16[128,2,128]{2,0,1:T(8,128)(2,1)}) %reduce-scatter.7.cloned.1.call-update) | async-done | bytes 65552 | tf_op jit(solution)/shard_map/reduce_scatter | solution.py:121
  45.6 0.9 copy.65
  46.6 3.3 %fusion = bf16[4096,256]{0,1:T(8,128)(2,1)} fusion(bf16[128,256]{0,1:T(8,128)(2,1)S(1)} %bitcast.101, bf16[1,128,4096]{2,1,0:T(8,128)(2,1)} %param.9), kind=kOutput, calls=%fused_computation.1 | convolution fusion | flops 269484032 | bytes 3211264 | tf_op jit(solution)/shard_map/td,te->de/dot_general | solution.py:134
  49.8 0.0 reduce-scatter.11.cloned.1.call-update
  49.8 0.0 reduce-scatter.5.cloned.1.call-start
  49.9 0.0 copy-done.3
  49.9 0.7 copy.57
  50.6 0.9 copy.58
  51.6 1.2 copy.89
  52.7 1.1 fusion.22
  53.9 1.0 copy.79
  54.8 5.8 %all_gather.13 = bf16[512,2,128]{2,0,1:T(8,128)(2,1)S(1)} all-gather(bf16[128,2,128]{2,0,1:T(8,128)(2,1)S(1)} %copy.58), channel_id=1, replica_groups=mesh['dp'=4,'ctx'=4,'tp'=2] {'ctx'}, dimensions={0}, use_global_device_ids=true | all-gather | bytes 327680 | tf_op jit(solution)/shard_map/all_gather | solution.py:113
  60.6 3.6 %fusion.2 = bf16[2,8,128,512]{2,3,1,0:T(8,128)(2,1)S(1)} fusion(f32[2,512,128,8]{2,1,3,0:T(8,128)} %copy-done.1, f32[2,8,128]{2,1,0:T(8,128)S(1)} %copy.79, f32[2,8,128]{2,1,0:T(8,128)S(1)} %bitcast.112, pred[128,512]{0,1:T(8,128)(4,1)} %copy-done.4, bf16[128,2,8,128]{3,2,1,0:T(8,128)(2,1)S(1)} %bitcast.98, bf16[512,2,128]{2,0,1:T(8,128)(2,1)S(1)} %all_gather.13), kind=kOutput, calls=%fused_computation.5 | convolution fusion | flops 274726912 | bytes 7159808 | tf_op jit(solution)/shard_map/tgjd,kgd->gjtk/dot_general | solution.py:62
  64.2 0.0 copy-start.2
  64.2 1.3 copy-done.2
  65.5 1.4 fusion.20
  66.9 0.0 reduce-scatter.5.cloned.1.call-update
  66.9 0.0 all-gather.3.cloned.1.call-start
  67.0 14.2 %reduce-scatter.11.cloned.1.call-done = bf16[1024,256]{0,1:T(8,128)(2,1)} async-done(((bf16[4096,256]{0,1:T(8,128)(2,1)}), bf16[1024,256]{0,1:T(8,128)(2,1)}) %reduce-scatter.11.cloned.1.call-update) | async-done | bytes 524304 | tf_op jit(solution)/shard_map/reduce_scatter | solution.py:135
  81.2 0.0 all-gather.3.cloned.1.call-update
  81.2 0.0 reduce-scatter.9.cloned.1.call-start
  81.2 0.0 copy-done
  81.3 1.8 convolution_convert_fusion.1
  83.0 0.0 reduce-scatter.9.cloned.1.call-update
  83.1 2.1 %fusion.9 = bf16[2,8,128,128]{2,3,1,0:T(8,128)(2,1)S(1)} fusion(bf16[2,8,128,512]{2,3,1,0:T(8,128)(2,1)} %copy-done.2, bf16[512,2,128]{2,0,1:T(8,128)(2,1)S(1)} %all_gather.12), kind=kOutput, calls=%fused_computation.13 | convolution fusion | flops 268959744 | bytes 2883584 | tf_op jit(solution)/shard_map/gjtk,kgd->tgjd/dot_general | solution.py:66
  85.2 1.0 copy.67
  86.2 18.1 %reduce-scatter.5.cloned.1.call-done = bf16[128,2,128]{2,0,1:T(8,128)(2,1)} async-done(((bf16[512,2,128]{2,0,1:T(8,128)(2,1)}), bf16[128,2,128]{2,0,1:T(8,128)(2,1)}) %reduce-scatter.5.cloned.1.call-update) | async-done | bytes 65552 | tf_op jit(solution)/shard_map/reduce_scatter | solution.py:118
  104.3 0.9 multiply_convert_fusion
  105.2 0.1 copy.63
  105.3 0.7 copy.68
  106.0 0.7 copy.69
  106.8 44.6 %all-gather.3.cloned.1.call-done = bf16[4096,256]{0,1:T(8,128)(2,1)} async-done(((bf16[1024,256]{0,1:T(8,128)(2,1)}), bf16[4096,256]{0,1:T(8,128)(2,1)}) %all-gather.3.cloned.1.call-update) | async-done | bytes 2097168 | tf_op jit(solution)/shard_map/all_gather | solution.py:143
  151.4 4.5 %reshape.118 = bf16[4,1024,256]{1,0,2:T(4,128)(2,1)} reshape(bf16[4096,256]{0,1:T(8,128)(2,1)} %all-gather.3.cloned.1.call-done) | data formatting | bytes 4194304 | tf_op jit(solution)/shard_map/all_gather | solution.py:143
  155.9 4.9 %reduce_sum.32 = bf16[1024,256]{0,1:T(8,128)(2,1)} reduce(bf16[4,1024,256]{1,0,2:T(4,128)(2,1)} %reshape.118, bf16[]{:T(256)} %constant.68.clone.1), dimensions={0}, to_apply=%region_6.7 | reduce | flops 786432 | bytes 2621442 | tf_op jit(solution)/shard_map/reduce_sum | solution.py:143
  160.9 1.2 convert_multiply_fusion.1
  162.0 1.3 copy.70
  163.3 10.0 %reduce-scatter.9.cloned.1.call-done = bf16[128,2048]{1,0:T(8,128)(2,1)} async-done(((bf16[128,4096]{1,0:T(8,128)(2,1)}), bf16[128,2048]{1,0:T(8,128)(2,1)}) %reduce-scatter.9.cloned.1.call-update) | async-done | bytes 524304 | tf_op jit(solution)/shard_map/reduce_scatter | solution.py:149
  (4 shorter events, 0.0 us)
Async XLA Ops:
  7.2 74.1 %copy-start = (bf16[4096,256]{1,0:T(8,128)(2,1)S(1)}, bf16[4096,256]{1,0:T(8,128)(2,1)}, u32[]{:S(2)}) copy-start(bf16[4096,256]{1,0:T(8,128)(2,1)} %param.17) | copy-start | bytes 6291460
  7.2 15.2 %copy-start.5 = (f32[1,16,128]{2,1,0:T(8,128)S(1)}, f32[1,16,128]{2,1,0:T(8,128)}, u32[]{:S(2)}) copy-start(f32[1,16,128]{2,1,0:T(8,128)} %param.15) | copy-start | bytes 24580
  7.2 38.4 %reduce-scatter.7.cloned.1.call-start = ((), (), s32[]{:S(2)}) async-start(), calls=%async_computation.5 | async-start | bytes 327680 | tf_op jit(solution)/shard_map/reduce_scatter | solution.py:121
  19.7 0.7 copy-start.4
  20.4 1.9 %copy-start.1 = (f32[2,512,128,8]{2,1,3,0:T(8,128)}, f32[2,512,128,8]{2,1,3,0:T(8,128)S(1)}, u32[]{:S(2)}) copy-start(f32[2,512,128,8]{2,1,3,0:T(8,128)S(1)} %fusion.26) | copy-start | bytes 12582916
  24.1 25.8 %copy-start.3 = (bf16[1,128,256]{2,1,0:T(8,128)(2,1)S(1)}, bf16[1,128,256]{2,1,0:T(8,128)(2,1)}, u32[]{:S(2)}) copy-start(bf16[1,128,256]{2,1,0:T(8,128)(2,1)} %param.12) | copy-start | bytes 196612
  24.1 57.0 %reduce-scatter.11.cloned.1.call-start = ((), (), s32[]{:S(2)}) async-start(), calls=%async_computation.7 | async-start | bytes 2621440 | tf_op jit(solution)/shard_map/reduce_scatter | solution.py:135
  49.8 54.5 %reduce-scatter.5.cloned.1.call-start = ((), (), s32[]{:S(2)}) async-start(), calls=%async_computation.4 | async-start | bytes 327680 | tf_op jit(solution)/shard_map/reduce_scatter | solution.py:118
  64.2 1.3 copy-start.2
  66.9 84.5 %all-gather.3.cloned.1.call-start = ((), (), s32[]{:S(2)}) async-start(), calls=%async_computation.8 | async-start | bytes 2621440 | tf_op jit(solution)/shard_map/all_gather | solution.py:143
  81.2 92.1 %reduce-scatter.9.cloned.1.call-start = ((), (), s32[]{:S(2)}) async-start(), calls=%async_computation.6 | async-start | bytes 1572864 | tf_op jit(solution)/shard_map/reduce_scatter | solution.py:149
Sparse Core Ops, SparseCore 0:
  24.2 21.3 reduce-scatter.6
  50.0 31.1 reduce-scatter.10
  84.2 20.0 reduce-scatter.4
  105.7 45.6 all-gather.2
  154.1 19.1 reduce-scatter.8
